TPU v7x, 128 devices: a whole 4x4x4 slice. The times are simulated.
128 devices in a mesh: trade: 16 (over z, x), path: 8 (over y, core).
Axes of the slice: x: 4, y: 4, z: 4, core: 2. Of those that a mesh axis runs over, the one named last changes fastest.
Arguments:
- coefficients: bfloat16 [32768, 256], P('trade'), may hold values from -6 to 6
- path_basis: bfloat16 [256, 4096], P(None, 'path'), may hold values from -6 to 6
- trade_owner: int32 [32768, 1], P('trade'), may hold values from 0 to 15; in each aligned block of 2048 rows (0 to 2047, 2048 to 4095, ...) at most 192 rows name the same one
- trade_slot: int32 [32768], P('trade'), may hold values from 0 to 63
- set_factor: int32 [1024], P('trade'), may hold values from 0 to 511
- set_level: int32 [1024], P('trade'), may hold values from 0 to 3
- default_date: int32 [512, 4096], P(None, 'path'), may hold values from 0 to 4
- discount: float32 [4], replicated, may hold values from 0.5 to 1
Outputs:
- alloc: float32 [32768], P('trade')
- set_cva: float32 [1024], P('trade')
Inputs may be any that keep to these rules, and one draw needn't show every extreme that they name: `trade_owner`: in the rows of one device no value is named by more than 192 rows, a bound that some block reaches.
All inputs are finite; a program needn't handle non-finite values.
Results may differ from a plain program's by a relative error of at most 0.0045.
Values may be sent and summed in bfloat16 or wider, within the bound.
A program may use at most 64 MiB of HBM per device.

v0:
```python
import jax
import jax.numpy as jnp
from jax import lax
from jax.experimental import pallas as pl
from jax.experimental.pallas import tpu as pltpu
from jax.sharding import PartitionSpec as P

MESH = pl.DeviceIdType.MESH
K = 64
DATES = 4
LANES = 128
level_step = 1.5


def grid_offsets(side):
    def far(step):
        return min(step, side - step)

    offsets = [(a, b) for a in range(side) for b in range(side)]
    return sorted(offsets, key=lambda o: -(far(o[0]) + far(o[1])))


def diagonal(rows, columns, first):
    at = lax.broadcasted_iota(jnp.int32, (rows, columns), 0) + first
    return at == lax.broadcasted_iota(jnp.int32, (rows, columns), 1)


def arrive(ref, sem):
    pltpu.make_async_copy(ref, ref, sem).wait()


def turned(x):
    size = x.shape[1]
    ones = jnp.where(diagonal(size, size, 0), 1.0, 0.0).astype(x.dtype)
    return lax.dot_general(
        ones, x, (((1,), (1,)), ((), ())), preferred_element_type=jnp.float32
    ).astype(x.dtype)


def make_kernel(n_trade, n_path, side, n_set, trades, per_path, factors):
    offsets = grid_offsets(side)
    n_along = n_path - 1
    count = n_set // 2
    sub = count // 2
    rows = n_trade * sub
    width = DATES * K
    path_steps = sorted(range(1, n_path), key=lambda k: -min(k, n_path - k))
    early = n_trade // 2 + 1
    tall = trades // LANES
    f32, bf16 = jnp.float32, jnp.bfloat16

    def kernel(
        coef_hbm, basis_hbm, owner_hbm, slot_hbm, factor_hbm, level_hbm, date_hbm, disc_hbm,
        alloc_ref, cva_ref,
        coef, coef_t, basis, basis_other, basis_t, where, sets, date, disc, onehot, dated, dated_other,
        cva_mine, cva_in, al_mine, al_in, part, arrived, gmine, gall,
        in_sem, s1, r1, sd, rd, s3, r3, sc, rc, sa, ra,
    ):
        me = lax.axis_index("trade")
        lane = lax.axis_index("path")
        core = lax.rem(lane, 2)
        partner = lane + 1 - 2 * core
        me_a, me_b = me // side, lax.rem(me, side)
        others = [
            lax.rem(me_a + a, side) * side + lax.rem(me_b + b, side) for a, b in offsets
        ]
        on_path = [lax.rem(lane + k, n_path) for k in path_steps]

        across = [{"trade": o, "path": partner} for o in others]
        first, first_sent = count * core, count * (1 - core)

        barrier = pltpu.get_barrier_semaphore()
        for there in across:
            pl.semaphore_signal(barrier, inc=1, device_id=there, device_id_type=MESH)
        for k, q in zip(path_steps, on_path):
            if k % 2 == 0:
                pl.semaphore_signal(barrier, inc=1, device_id={"path": q}, device_id_type=MESH)
        for y in range(1, n_path // 2):
            q = lax.rem(partner + 2 * y, n_path)
            pl.semaphore_signal(barrier, inc=1, device_id={"path": q}, device_id_type=MESH)
        for src, dst, i in (
            (owner_hbm, where.at[0], 0), (slot_hbm, where.at[1], 0), (coef_hbm, coef, 1),
            (basis_hbm, basis, 2), (factor_hbm, sets.at[0], 3), (level_hbm, sets.at[1], 3),
            (disc_hbm, disc, 4), (date_hbm, date, 5),
        ):
            pltpu.make_async_copy(src, dst, in_sem.at[i]).start()

        def send(src, dst, send_sem, recv_sem, device):
            pltpu.make_async_remote_copy(
                src_ref=src, dst_ref=dst, send_sem=send_sem, recv_sem=recv_sem,
                device_id=device, device_id_type=MESH,
            ).start()

        arrive(where, in_sem.at[0])
        loc = where[1] - first_sent
        ids = jnp.where(
            (loc >= 0) & (loc < count), (loc // sub) * rows + where[0] * sub + lax.rem(loc, sub), -1
        )
        which = lax.broadcasted_iota(jnp.int32, (2 * rows, LANES), 0)
        for r in range(tall):
            hit = which == ids[r : r + 1, :]
            onehot[:, r * LANES : (r + 1) * LANES] = jnp.where(hit, 1.0, 0.0).astype(bf16)
        arrive(coef, in_sem.at[1])
        sums = jnp.dot(onehot[...], coef[...], preferred_element_type=f32)
        part[...] = sums.astype(bf16).reshape(2, n_trade, sub, width)

        arrive(basis, in_sem.at[2])
        pl.semaphore_wait(barrier, n_trade + n_path - 2)
        for h in range(2):
            for j, (o, there) in enumerate(zip(others, across)):
                group = 0 if j < early else 1
                send(part.at[h, o], arrived.at[h, j], s1.at[0], r1.at[2 * h + group], there)
        send(basis, basis_other, sd.at[0], rd.at[0], {"path": partner})

        arrive(sets, in_sem.at[3])
        arrive(disc, in_sem.at[4])
        limit = level_step * jnp.sum(
            jnp.where(diagonal(count, n_set, first), sets[1].astype(f32), 0.0),
            axis=1, keepdims=True,
        )
        wanted = jnp.sum(
            jnp.where(diagonal(n_set, n_set, 0), sets[0].astype(f32), 0.0),
            axis=1, keepdims=True,
        )
        pick = lax.broadcasted_iota(jnp.int32, (n_set, factors), 1).astype(f32) == wanted
        pick = jnp.where(pick, 1.0, 0.0).astype(bf16)
        arrive(date, in_sem.at[5])
        dated[...] = jnp.dot(
            pick, date[...].astype(f32).astype(bf16), preferred_element_type=f32
        ).reshape(2, count, per_path)
        send(dated.at[1 - core], dated_other, sd.at[1], rd.at[1], {"path": partner})
        coef_t[...] = turned(coef[...])
        basis_t[0] = turned(basis[...])
        arrive(basis_other, rd.at[0])
        basis_t[1] = turned(basis_other[...])
        arrive(dated_other, rd.at[1])

        moment_of = lax.broadcasted_iota(jnp.int32, (sub, width), 1) // K
        cvas = []
        for h in range(2):
            some_sets = slice(h * sub, (h + 1) * sub)
            total = jnp.zeros((sub, width), f32)
            for group, some in ((1, range(early, n_trade)), (0, range(early))):
                arrive(arrived.at[h, some.start : some.stop], r1.at[2 * h + group])
                for j in some:
                    total = total + arrived[h, j].astype(f32)
            stack = jnp.concatenate([jnp.where(moment_of == d, total, 0.0) for d in range(DATES)])
            high = stack.astype(bf16)
            low = (stack - high.astype(f32)).astype(bf16)
            cva = jnp.zeros((sub, 1), f32)
            grads = 0.0
            for i, (b_ref, when) in enumerate(
                ((basis, dated[core, some_sets]), (basis_other, dated_other[some_sets]))
            ):
                b = b_ref[...]
                netted = jnp.dot(high, b, preferred_element_type=f32) + jnp.dot(
                    low, b, preferred_element_type=f32
                )
                slopes = []
                for d in range(DATES):
                    x = netted[d * sub : (d + 1) * sub] - limit[some_sets]
                    e = jnp.exp(-jnp.abs(x))
                    inv = 1.0 / (1.0 + e)
                    plus = jnp.maximum(x, 0.0) + jnp.log1p(e)
                    sig = jnp.where(x >= 0, inv, e * inv)
                    factor_d = disc[0:1, d : d + 1] / (per_path * n_path)
                    weight = jnp.where(when == float(d), factor_d, 0.0)
                    cva = cva + jnp.sum(weight * plus, axis=1, keepdims=True)
                    slopes.append(weight * sig)
                grads = grads + jnp.dot(
                    jnp.concatenate(slopes).astype(bf16), basis_t[i], preferred_element_type=f32
                )
            cvas.append(cva)
            grad = jnp.zeros((sub, width), f32)
            for d in range(DATES):
                grad = grad + jnp.where(moment_of == d, grads[d * sub : (d + 1) * sub], 0.0)
            gmine[h] = grad.astype(bf16)
            for there in across:
                send(gmine.at[h], gall.at[h, me], s3.at[0], r3.at[h], there)
        cva = jnp.concatenate(cvas)
        cva_mine[...] = jnp.sum(
            jnp.where(diagonal(count, n_set, first), cva, 0.0), axis=0, keepdims=True
        )
        for j, q in enumerate(on_path):
            send(cva_mine, cva_in.at[j], sc.at[0], rc.at[0], {"path": q})

        block = 2 * LANES
        for h in range(2):
            arrive(gall.at[h], r3.at[h])
            g = gall[h].reshape(rows, width)
            which = lax.broadcasted_iota(jnp.int32, (rows, LANES), 0) + h * rows
            for r in range(trades // block):
                dots = jnp.dot(
                    g, coef_t[:, r * block : (r + 1) * block], preferred_element_type=f32
                )
                for i in range(2):
                    at = 2 * r + i
                    hit = which == ids[at : at + 1, :]
                    share = jnp.sum(
                        jnp.where(hit, dots[:, i * LANES : (i + 1) * LANES], 0.0),
                        axis=0, keepdims=True,
                    )
                    if h == 0:
                        al_mine[at // 8, at % 8 : at % 8 + 1, :] = share
                    else:
                        al_mine[at // 8, at % 8 : at % 8 + 1, :] += share
                if h == 1 and (2 * r + 2) % 8 == 0:
                    i = (2 * r + 2) // 8 - 1
                    for j, q in enumerate(on_path):
                        send(al_mine.at[i], al_in.at[i, j], sa.at[0], ra.at[i], {"path": q})
        arrive(arrived, s1.at[0])
        arrive(arrived, s3.at[0])
        arrive(basis, sd.at[0])
        arrive(dated_other, sd.at[1])
        arrive(cva_in, sc.at[0])


        arrive(cva_in, rc.at[0])
        cva_total = cva_mine[...]
        for j in range(n_along):
            cva_total = cva_total + cva_in[j]
        cva_ref[...] = cva_total
        for i in range(tall // 8):
            arrive(al_in.at[i], ra.at[i])
            total_alloc = al_mine[i]
            for j in range(n_along):
                total_alloc = total_alloc + al_in[i, j]
            alloc_ref[i * 8 : (i + 1) * 8] = total_alloc
        arrive(al_in, sa.at[0])

    return kernel


def write_out(alloc, cva, alloc_out, cva_out, sem):
    copies = [
        pltpu.make_async_copy(src, dst, sem.at[i])
        for i, (src, dst) in enumerate(((alloc, alloc_out), (cva, cva_out)))
    ]
    for copy in copies:
        copy.start()
    for copy in copies:
        copy.wait()


def solution(mesh):
    n_trade, n_path = mesh.shape["trade"], mesh.shape["path"]
    side = 4

    def on_device(
        coefficients, path_basis, trade_owner, trade_slot, set_factor, set_level, default_date,
        discount,
    ):
        trades, width = coefficients.shape
        n_set = set_factor.shape[0]
        factors, per_path = default_date.shape
        tall = trades // LANES
        half = n_set // 2
        bf16, f32, i32 = jnp.bfloat16, jnp.float32, jnp.int32
        dma = pltpu.SemaphoreType.DMA
        alloc, cva = pl.pallas_call(
            make_kernel(n_trade, n_path, side, n_set, trades, per_path, factors),
            out_shape=(pltpu.VMEM((tall, LANES), f32), pltpu.VMEM((1, n_set), f32)),
            in_specs=[pl.BlockSpec(memory_space=pl.ANY)] * 8,
            out_specs=(
                pl.BlockSpec(memory_space=pltpu.VMEM),
                pl.BlockSpec(memory_space=pltpu.VMEM),
            ),
            scratch_shapes=[
                pltpu.VMEM((trades, width), bf16),
                pltpu.VMEM((width, trades), bf16),
                pltpu.VMEM((width, per_path), bf16),
                pltpu.VMEM((width, per_path), bf16),
                pltpu.VMEM((2, per_path, width), bf16),
                pltpu.VMEM((2, tall, LANES), i32),
                pltpu.VMEM((2, 1, n_set), i32),
                pltpu.VMEM((factors, per_path), i32),
                pltpu.VMEM((1, DATES), f32),
                pltpu.VMEM((n_trade * half, trades), bf16),
                pltpu.VMEM((2, half, per_path), f32),
                pltpu.VMEM((half, per_path), f32),
                pltpu.VMEM((1, n_set), f32),
                pltpu.VMEM((n_path - 1, 1, n_set), f32),
                pltpu.VMEM((tall // 8, 8, LANES), f32),
                pltpu.VMEM((tall // 8, n_path - 1, 8, LANES), f32),
                pltpu.VMEM((2, n_trade, half // 2, width), bf16),
                pltpu.VMEM((2, n_trade, half // 2, width), bf16),
                pltpu.VMEM((2, half // 2, width), bf16),
                pltpu.VMEM((2, n_trade, half // 2, width), bf16),
                dma((6,)),
                dma((1,)),
                dma((4,)),
                dma((2,)),
                dma((2,)),
                dma((1,)),
                dma((2,)),
                dma((1,)),
                dma((1,)),
                dma((1,)),
                dma((2,)),
            ],
            compiler_params=pltpu.CompilerParams(collective_id=0, has_side_effects=True),
        )(
            coefficients,
            path_basis,
            trade_owner.reshape(tall, LANES),
            trade_slot.reshape(tall, LANES),
            set_factor.reshape(1, n_set),
            set_level.reshape(1, n_set),
            default_date,
            discount.reshape(1, DATES),
        )
        alloc, cva = pl.pallas_call(
            write_out,
            out_shape=(
                jax.ShapeDtypeStruct((tall, LANES), f32),
                jax.ShapeDtypeStruct((1, n_set), f32),
            ),
            in_specs=[pl.BlockSpec(memory_space=pltpu.VMEM)] * 2,
            out_specs=(
                pl.BlockSpec(memory_space=pltpu.HBM),
                pl.BlockSpec(memory_space=pltpu.HBM),
            ),
            scratch_shapes=[dma((2,))],
            compiler_params=pltpu.CompilerParams(vmem_limit_bytes=1 << 20),
        )(alloc, cva)
        return alloc.reshape(trades), cva.reshape(n_set)

    return jax.shard_map(
        on_device,
        mesh=mesh,
        in_specs=(
            P("trade", None),
            P(None, "path"),
            P("trade", None),
            P("trade"),
            P("trade"),
            P("trade"),
            P(None, "path"),
            P(),
        ),
        out_specs=(P("trade"), P("trade")),
        check_vma=False,
    )
```

profile of v0, /device:TPU:1, one launch (start us, length us, event | category | flops | bytes accessed | tf_op | source)
XLA Modules:
  0.0 25.6 jit_solution(8465508849718072450)
XLA Ops:
  0.6 24.3 %shard_map.95 = (f32[16,128]{1,0:T(8,128)S(1)}, f32[1,64]{1,0:T(1,128)S(1)}) custom-call(bf16[2048,256]{1,0:T(8,128)(2,1)} %coef_hbm.1, bf16[256,512]{1,0:T(8,128)(2,1)} %basis_hbm.1, s32[16,128]{1,0:T(8,128)} %bitcast.7, s32[16,128]{1,0:T(8,128)} %bitcast.8, s32[1,64]{1,0:T(1,128)} %bitcast.9, s32[1,64]{1,0:T(1,128)} %bitcast.10, s32[512,512]{1,0:T(8,128)} %date_hbm.1, ...), custom_call_target="tpu_custom_call" | custom-call | tf_op jit(solution)/shard_map/pallas_call | solution.py:260
  25.0 0.6 %shard_map.96 = (f32[16,128]{1,0:T(8,128)}, f32[1,64]{1,0:T(1,128)}) custom-call(f32[16,128]{1,0:T(8,128)S(1)} %get-tuple-element.6.alloc, f32[1,64]{1,0:T(1,128)S(1)} %get-tuple-element.7.cva), custom_call_target="tpu_custom_call" | custom-call | tf_op jit(solution)/shard_map/pallas_call | solution.py:312
where the time goes:
time: 25.7 us; the launch traced here: 25.6 us
  Pallas kernels  25 us (97%)
  between operations  0.64 us (2%)
    pallas_call x1, Pallas kernels, on_device(): pl.pallas_call(make_kernel(n_trade, n_path, side, n_set, trades, per_path...  24.3 us
    pallas_call x1, Pallas kernels, on_device(): pl.pallas_call(write_out, out_shape=(jax.ShapeDtypeStruct((tall, LANES),...  0.62 us

commit v1 on v0

--- a/solution.py
+++ b/solution.py
@@ -17,7 +17,7 @@
         return min(step, side - step)
 
     offsets = [(a, b) for a in range(side) for b in range(side)]
-    return sorted(offsets, key=lambda o: -(far(o[0]) + far(o[1])))
+    return sorted(offsets, key=lambda o: (-(far(o[0]) + far(o[1])), (o[0] + 2 * o[1]) % 4, o[0]))
 
 
 def diagonal(rows, columns, first):
@@ -44,7 +44,7 @@
     sub = count // 2
     rows = n_trade * sub
     width = DATES * K
-    path_steps = sorted(range(1, n_path), key=lambda k: -min(k, n_path - k))
+    path_steps = sorted(range(1, n_path), key=lambda k: (2, 4, 3, 5, 6, 7, 1).index(k))
     early = n_trade // 2 + 1
     tall = trades // LANES
     f32, bf16 = jnp.float32, jnp.bfloat16
@@ -52,7 +52,7 @@
     def kernel(
         coef_hbm, basis_hbm, owner_hbm, slot_hbm, factor_hbm, level_hbm, date_hbm, disc_hbm,
         alloc_ref, cva_ref,
-        coef, coef_t, basis, basis_other, basis_t, where, sets, date, disc, onehot, dated, dated_other,
+        coef, coef_t, basis, basis_other, basis_t, where, sets, date, disc, onehot, dated, dated_other, excess, weights,
         cva_mine, cva_in, al_mine, al_in, part, arrived, gmine, gall,
         in_sem, s1, r1, sd, rd, s3, r3, sc, rc, sa, ra,
     ):
@@ -69,6 +69,16 @@
         across = [{"trade": o, "path": partner} for o in others]
         first, first_sent = count * core, count * (1 - core)
 
+        loads = [
+            pltpu.make_async_copy(src, dst, in_sem.at[i])
+            for src, dst, i in (
+                (owner_hbm, where.at[0], 0), (slot_hbm, where.at[1], 0), (coef_hbm, coef, 1),
+                (basis_hbm, basis, 2), (factor_hbm, sets.at[0], 3), (level_hbm, sets.at[1], 3),
+                (disc_hbm, disc, 4), (date_hbm, date, 5),
+            )
+        ]
+        for load in loads[:3]:
+            load.start()
         barrier = pltpu.get_barrier_semaphore()
         for there in across:
             pl.semaphore_signal(barrier, inc=1, device_id=there, device_id_type=MESH)
@@ -78,12 +88,8 @@
         for y in range(1, n_path // 2):
             q = lax.rem(partner + 2 * y, n_path)
             pl.semaphore_signal(barrier, inc=1, device_id={"path": q}, device_id_type=MESH)
-        for src, dst, i in (
-            (owner_hbm, where.at[0], 0), (slot_hbm, where.at[1], 0), (coef_hbm, coef, 1),
-            (basis_hbm, basis, 2), (factor_hbm, sets.at[0], 3), (level_hbm, sets.at[1], 3),
-            (disc_hbm, disc, 4), (date_hbm, date, 5),
-        ):
-            pltpu.make_async_copy(src, dst, in_sem.at[i]).start()
+        for load in loads[3:]:
+            load.start()
 
         def send(src, dst, send_sem, recv_sem, device):
             pltpu.make_async_remote_copy(
@@ -97,11 +103,31 @@
             (loc >= 0) & (loc < count), (loc // sub) * rows + where[0] * sub + lax.rem(loc, sub), -1
         )
         which = lax.broadcasted_iota(jnp.int32, (2 * rows, LANES), 0)
-        for r in range(tall):
-            hit = which == ids[r : r + 1, :]
-            onehot[:, r * LANES : (r + 1) * LANES] = jnp.where(hit, 1.0, 0.0).astype(bf16)
+        places = lax.broadcasted_iota(jnp.int32, (rows, LANES), 0).astype(f32).astype(bf16)
+        one, none = jnp.ones((rows, LANES), bf16), jnp.zeros((rows, LANES), bf16)
+        local = [
+            jnp.where((ids >= h * rows) & (ids < (h + 1) * rows), ids - h * rows, -1).astype(f32)
+            for h in range(2)
+        ]
+
+        def picked(h, r):
+            row = jnp.broadcast_to(local[h][r : r + 1, :], (16, LANES)).astype(bf16)
+            return jnp.where(places == jnp.concatenate([row] * (rows // 16)), one, none)
+
         arrive(coef, in_sem.at[1])
-        sums = jnp.dot(onehot[...], coef[...], preferred_element_type=f32)
+        deep = tall // 2
+        sums = 0.0
+        for q in range(2):
+            tile = jnp.concatenate(
+                [
+                    jnp.concatenate([picked(h, r) for r in range(q * deep, (q + 1) * deep)], axis=1)
+                    for h in range(2)
+                ]
+            )
+            sums = sums + jnp.dot(
+                tile, coef[q * deep * LANES : (q + 1) * deep * LANES, :],
+                preferred_element_type=f32,
+            )
         part[...] = sums.astype(bf16).reshape(2, n_trade, sub, width)
 
         arrive(basis, in_sem.at[2])
@@ -136,7 +162,6 @@
         arrive(dated_other, rd.at[1])
 
         moment_of = lax.broadcasted_iota(jnp.int32, (sub, width), 1) // K
-        cvas = []
         for h in range(2):
             some_sets = slice(h * sub, (h + 1) * sub)
             total = jnp.zeros((sub, width), f32)
@@ -147,7 +172,6 @@
             stack = jnp.concatenate([jnp.where(moment_of == d, total, 0.0) for d in range(DATES)])
             high = stack.astype(bf16)
             low = (stack - high.astype(f32)).astype(bf16)
-            cva = jnp.zeros((sub, 1), f32)
             grads = 0.0
             for i, (b_ref, when) in enumerate(
                 ((basis, dated[core, some_sets]), (basis_other, dated_other[some_sets]))
@@ -161,22 +185,30 @@
                     x = netted[d * sub : (d + 1) * sub] - limit[some_sets]
                     e = jnp.exp(-jnp.abs(x))
                     inv = 1.0 / (1.0 + e)
-                    plus = jnp.maximum(x, 0.0) + jnp.log1p(e)
                     sig = jnp.where(x >= 0, inv, e * inv)
                     factor_d = disc[0:1, d : d + 1] / (per_path * n_path)
                     weight = jnp.where(when == float(d), factor_d, 0.0)
-                    cva = cva + jnp.sum(weight * plus, axis=1, keepdims=True)
+                    excess[h, DATES * i + d] = x
+                    weights[h, DATES * i + d] = weight
                     slopes.append(weight * sig)
                 grads = grads + jnp.dot(
                     jnp.concatenate(slopes).astype(bf16), basis_t[i], preferred_element_type=f32
                 )
-            cvas.append(cva)
             grad = jnp.zeros((sub, width), f32)
             for d in range(DATES):
                 grad = grad + jnp.where(moment_of == d, grads[d * sub : (d + 1) * sub], 0.0)
             gmine[h] = grad.astype(bf16)
-            for there in across:
+            for o in [0, 10, 6, 9, 11, 14, 2, 5, 7, 8, 13, 15, 1, 3, 4, 12]:
+                there = {"trade": o, "path": partner}
                 send(gmine.at[h], gall.at[h, me], s3.at[0], r3.at[h], there)
+        cvas = []
+        for h in range(2):
+            cva = jnp.zeros((sub, per_path), f32)
+            for i in range(2 * DATES):
+                x = excess[h, i]
+                plus = jnp.maximum(x, 0.0) + jnp.log1p(jnp.exp(-jnp.abs(x)))
+                cva = cva + weights[h, i] * plus
+            cvas.append(jnp.sum(cva, axis=1, keepdims=True))
         cva = jnp.concatenate(cvas)
         cva_mine[...] = jnp.sum(
             jnp.where(diagonal(count, n_set, first), cva, 0.0), axis=0, keepdims=True
@@ -278,6 +310,8 @@
                 pltpu.VMEM((n_trade * half, trades), bf16),
                 pltpu.VMEM((2, half, per_path), f32),
                 pltpu.VMEM((half, per_path), f32),
+                pltpu.VMEM((2, 2 * DATES, half // 2, per_path), f32),
+                pltpu.VMEM((2, 2 * DATES, half // 2, per_path), f32),
                 pltpu.VMEM((1, n_set), f32),
                 pltpu.VMEM((n_path - 1, 1, n_set), f32),
                 pltpu.VMEM((tall // 8, 8, LANES), f32),

time: 25.7 us -> 25.4 us (0.988)
  Pallas kernels: 25 us -> 24.7 us
    pallas_call x1, Pallas kernels: 24.3 us -> 24 us  [on_device(): pl.pallas_call(make_kernel(n_trade, n_path, side, n_set, trades, per_path...]
where the time goes in v1:
time: 25.4 us; the launch traced here: 25.3 us
  Pallas kernels  24.7 us (97%)
  between operations  0.64 us (3%)
    pallas_call x1, Pallas kernels, on_device(): pl.pallas_call(make_kernel(n_trade, n_path, side, n_set, trades, per_path...  24 us
    pallas_call x1, Pallas kernels, on_device(): pl.pallas_call(write_out, out_shape=(jax.ShapeDtypeStruct((tall, LANES),...  0.62 us

profile of v1, /device:TPU:1, one launch (start us, length us, event | category | flops | bytes accessed | tf_op | source)
XLA Modules:
  0.0 25.3 jit_solution(14851409638581205398)
XLA Ops:
  0.6 24.0 %shard_map.95 = (f32[16,128]{1,0:T(8,128)S(1)}, f32[1,64]{1,0:T(1,128)S(1)}) custom-call(bf16[2048,256]{1,0:T(8,128)(2,1)} %coef_hbm.1, bf16[256,512]{1,0:T(8,128)(2,1)} %basis_hbm.1, s32[16,128]{1,0:T(8,128)} %bitcast.7, s32[16,128]{1,0:T(8,128)} %bitcast.8, s32[1,64]{1,0:T(1,128)} %bitcast.9, s32[1,64]{1,0:T(1,128)} %bitcast.10, s32[512,512]{1,0:T(8,128)} %date_hbm.1, ...), custom_call_target="tpu_custom_call" | custom-call | tf_op jit(solution)/shard_map/pallas_call | solution.py:292
  24.7 0.6 %shard_map.96 = (f32[16,128]{1,0:T(8,128)}, f32[1,64]{1,0:T(1,128)}) custom-call(f32[16,128]{1,0:T(8,128)S(1)} %get-tuple-element.6.alloc, f32[1,64]{1,0:T(1,128)S(1)} %get-tuple-element.7.cva), custom_call_target="tpu_custom_call" | custom-call | tf_op jit(solution)/shard_map/pallas_call | solution.py:346

commit v2 on v1

--- a/solution.py
+++ b/solution.py
@@ -134,8 +134,8 @@
         pl.semaphore_wait(barrier, n_trade + n_path - 2)
         for h in range(2):
             for j, (o, there) in enumerate(zip(others, across)):
-                group = 0 if j < early else 1
-                send(part.at[h, o], arrived.at[h, j], s1.at[0], r1.at[2 * h + group], there)
+                group = 0
+                send(part.at[h, o], arrived.at[h, j], s1.at[0], r1.at[h], there)
         send(basis, basis_other, sd.at[0], rd.at[0], {"path": partner})
 
         arrive(sets, in_sem.at[3])
@@ -165,21 +165,23 @@
         for h in range(2):
             some_sets = slice(h * sub, (h + 1) * sub)
             total = jnp.zeros((sub, width), f32)
-            for group, some in ((1, range(early, n_trade)), (0, range(early))):
-                arrive(arrived.at[h, some.start : some.stop], r1.at[2 * h + group])
+            for group, some in ((0, range(n_trade)),):
+                arrive(arrived.at[h, some.start : some.stop], r1.at[h])
                 for j in some:
                     total = total + arrived[h, j].astype(f32)
-            stack = jnp.concatenate([jnp.where(moment_of == d, total, 0.0) for d in range(DATES)])
-            high = stack.astype(bf16)
-            low = (stack - high.astype(f32)).astype(bf16)
+            high = total.astype(bf16)
+            low = (total - high.astype(f32)).astype(bf16)
+            nothing = jnp.zeros_like(high)
+            stack = jnp.concatenate(
+                [jnp.where(moment_of == d, x, nothing) for x in (high, low) for d in range(DATES)]
+            )
             grads = 0.0
             for i, (b_ref, when) in enumerate(
                 ((basis, dated[core, some_sets]), (basis_other, dated_other[some_sets]))
             ):
                 b = b_ref[...]
-                netted = jnp.dot(high, b, preferred_element_type=f32) + jnp.dot(
-                    low, b, preferred_element_type=f32
-                )
+                netted = jnp.dot(stack, b, preferred_element_type=f32)
+                netted = netted[: DATES * sub] + netted[DATES * sub :]
                 slopes = []
                 for d in range(DATES):
                     x = netted[d * sub : (d + 1) * sub] - limit[some_sets]
@@ -322,7 +324,7 @@
                 pltpu.VMEM((2, n_trade, half // 2, width), bf16),
                 dma((6,)),
                 dma((1,)),
-                dma((4,)),
+                dma((2,)),
                 dma((2,)),
                 dma((2,)),
                 dma((1,)),

time: 25.4 us -> 25.3 us (level)
  no operation moved by 1% of the time
where the time goes in v2:
time: 25.3 us; the launch traced here: 25.2 us
  Pallas kernels  24.6 us (97%)
  between operations  0.64 us (3%)
    pallas_call x1, Pallas kernels, on_device(): pl.pallas_call(make_kernel(n_trade, n_path, side, n_set, trades, per_path...  23.9 us
    pallas_call x1, Pallas kernels, on_device(): pl.pallas_call(write_out, out_shape=(jax.ShapeDtypeStruct((tall, LANES),...  0.62 us

profile of v2, /device:TPU:1, one launch (start us, length us, event | category | flops | bytes accessed | tf_op | source)
XLA Modules:
  0.0 25.2 jit_solution(805613324377151479)
XLA Ops:
  0.6 23.9 %shard_map.95 = (f32[16,128]{1,0:T(8,128)S(1)}, f32[1,64]{1,0:T(1,128)S(1)}) custom-call(bf16[2048,256]{1,0:T(8,128)(2,1)} %coef_hbm.1, bf16[256,512]{1,0:T(8,128)(2,1)} %basis_hbm.1, s32[16,128]{1,0:T(8,128)} %bitcast.7, s32[16,128]{1,0:T(8,128)} %bitcast.8, s32[1,64]{1,0:T(1,128)} %bitcast.9, s32[1,64]{1,0:T(1,128)} %bitcast.10, s32[512,512]{1,0:T(8,128)} %date_hbm.1, ...), custom_call_target="tpu_custom_call" | custom-call | tf_op jit(solution)/shard_map/pallas_call | solution.py:294
  24.6 0.6 %shard_map.96 = (f32[16,128]{1,0:T(8,128)}, f32[1,64]{1,0:T(1,128)}) custom-call(f32[16,128]{1,0:T(8,128)S(1)} %get-tuple-element.6.alloc, f32[1,64]{1,0:T(1,128)S(1)} %get-tuple-element.7.cva), custom_call_target="tpu_custom_call" | custom-call | tf_op jit(solution)/shard_map/pallas_call | solution.py:348

commit v3 on v2

--- a/solution.py
+++ b/solution.py
@@ -17,7 +17,7 @@
         return min(step, side - step)
 
     offsets = [(a, b) for a in range(side) for b in range(side)]
-    return sorted(offsets, key=lambda o: (-(far(o[0]) + far(o[1])), (o[0] + 2 * o[1]) % 4, o[0]))
+    return sorted(offsets, key=lambda o: (-(far(o[0]) + far(o[1])), (o[0] + o[1]) % 4, -o[0]))
 
 
 def diagonal(rows, columns, first):
@@ -52,7 +52,7 @@
     def kernel(
         coef_hbm, basis_hbm, owner_hbm, slot_hbm, factor_hbm, level_hbm, date_hbm, disc_hbm,
         alloc_ref, cva_ref,
-        coef, coef_t, basis, basis_other, basis_t, where, sets, date, disc, onehot, dated, dated_other, excess, weights,
+        coef, coef_t, basis, basis_other, basis_t, where, sets, date, disc, dated, dated_other, excess, weights,
         cva_mine, cva_in, al_mine, al_in, part, arrived, gmine, gall,
         in_sem, s1, r1, sd, rd, s3, r3, sc, rc, sa, ra,
     ):
@@ -309,7 +309,6 @@
                 pltpu.VMEM((2, 1, n_set), i32),
                 pltpu.VMEM((factors, per_path), i32),
                 pltpu.VMEM((1, DATES), f32),
-                pltpu.VMEM((n_trade * half, trades), bf16),
                 pltpu.VMEM((2, half, per_path), f32),
                 pltpu.VMEM((half, per_path), f32),
                 pltpu.VMEM((2, 2 * DATES, half // 2, per_path), f32),

time: 25.3 us -> 25.4 us (level)
  no operation moved by 1% of the time
where the time goes in v3:
time: 25.4 us; the launch traced here: 25.2 us
  Pallas kernels  24.6 us (97%)
  between operations  0.64 us (3%)
    pallas_call x1, Pallas kernels, on_device(): pl.pallas_call(make_kernel(n_trade, n_path, side, n_set, trades, per_path...  24 us
    pallas_call x1, Pallas kernels, on_device(): pl.pallas_call(write_out, out_shape=(jax.ShapeDtypeStruct((tall, LANES),...  0.62 us

profile of v3, /device:TPU:1, one launch (start us, length us, event | category | flops | bytes accessed | tf_op | source)
XLA Modules:
  0.0 25.2 jit_solution(5004790264516789226)
XLA Ops:
  0.6 24.0 %shard_map.95 = (f32[16,128]{1,0:T(8,128)S(1)}, f32[1,64]{1,0:T(1,128)S(1)}) custom-call(bf16[2048,256]{1,0:T(8,128)(2,1)} %coef_hbm.1, bf16[256,512]{1,0:T(8,128)(2,1)} %basis_hbm.1, s32[16,128]{1,0:T(8,128)} %bitcast.7, s32[16,128]{1,0:T(8,128)} %bitcast.8, s32[1,64]{1,0:T(1,128)} %bitcast.9, s32[1,64]{1,0:T(1,128)} %bitcast.10, s32[512,512]{1,0:T(8,128)} %date_hbm.1, ...), custom_call_target="tpu_custom_call" | custom-call | tf_op jit(solution)/shard_map/pallas_call | solution.py:294
  24.6 0.6 %shard_map.96 = (f32[16,128]{1,0:T(8,128)}, f32[1,64]{1,0:T(1,128)}) custom-call(f32[16,128]{1,0:T(8,128)S(1)} %get-tuple-element.6.alloc, f32[1,64]{1,0:T(1,128)S(1)} %get-tuple-element.7.cva), custom_call_target="tpu_custom_call" | custom-call | tf_op jit(solution)/shard_map/pallas_call | solution.py:347

commit v4 on v3

--- a/solution.py
+++ b/solution.py
@@ -17,7 +17,7 @@
         return min(step, side - step)
 
     offsets = [(a, b) for a in range(side) for b in range(side)]
-    return sorted(offsets, key=lambda o: (-(far(o[0]) + far(o[1])), (o[0] + o[1]) % 4, -o[0]))
+    return sorted(offsets, key=lambda o: (-(far(o[0]) + far(o[1])), (o[0] + 2 * o[1]) % 4, o[0]))
 
 
 def diagonal(rows, columns, first):
@@ -77,8 +77,6 @@
                 (disc_hbm, disc, 4), (date_hbm, date, 5),
             )
         ]
-        for load in loads[:3]:
-            load.start()
         barrier = pltpu.get_barrier_semaphore()
         for there in across:
             pl.semaphore_signal(barrier, inc=1, device_id=there, device_id_type=MESH)
@@ -88,7 +86,7 @@
         for y in range(1, n_path // 2):
             q = lax.rem(partner + 2 * y, n_path)
             pl.semaphore_signal(barrier, inc=1, device_id={"path": q}, device_id_type=MESH)
-        for load in loads[3:]:
+        for load in loads:
             load.start()
 
         def send(src, dst, send_sem, recv_sem, device):

time: 25.4 us -> 25.3 us (level)
  no operation moved by 1% of the time
where the time goes in v4:
time: 25.3 us; the launch traced here: 25.2 us
  Pallas kernels  24.6 us (97%)
  between operations  0.64 us (3%)
    pallas_call x1, Pallas kernels, on_device(): pl.pallas_call(make_kernel(n_trade, n_path, side, n_set, trades, per_path...  23.9 us
    pallas_call x1, Pallas kernels, on_device(): pl.pallas_call(write_out, out_shape=(jax.ShapeDtypeStruct((tall, LANES),...  0.62 us

profile of v4, /device:TPU:1, one launch (start us, length us, event | category | flops | bytes accessed | tf_op | source)
XLA Modules:
  0.0 25.2 jit_solution(7360338996189624934)
XLA Ops:
  0.6 23.9 %shard_map.95 = (f32[16,128]{1,0:T(8,128)S(1)}, f32[1,64]{1,0:T(1,128)S(1)}) custom-call(bf16[2048,256]{1,0:T(8,128)(2,1)} %coef_hbm.1, bf16[256,512]{1,0:T(8,128)(2,1)} %basis_hbm.1, s32[16,128]{1,0:T(8,128)} %bitcast.7, s32[16,128]{1,0:T(8,128)} %bitcast.8, s32[1,64]{1,0:T(1,128)} %bitcast.9, s32[1,64]{1,0:T(1,128)} %bitcast.10, s32[512,512]{1,0:T(8,128)} %date_hbm.1, ...), custom_call_target="tpu_custom_call" | custom-call | tf_op jit(solution)/shard_map/pallas_call | solution.py:292
  24.6 0.6 %shard_map.96 = (f32[16,128]{1,0:T(8,128)}, f32[1,64]{1,0:T(1,128)}) custom-call(f32[16,128]{1,0:T(8,128)S(1)} %get-tuple-element.6.alloc, f32[1,64]{1,0:T(1,128)S(1)} %get-tuple-element.7.cva), custom_call_target="tpu_custom_call" | custom-call | tf_op jit(solution)/shard_map/pallas_call | solution.py:345
